TPU v7x, 512 devices: a whole 4x8x8 slice. The times are simulated.
512 devices in a mesh: row: 16 (over x_hi, y), col: 32 (over x_lo, z, core).
Axes of the slice: x: 4 (x_hi: 2, x_lo: 2; x = x_hi * 2 + x_lo), y: 8, z: 8, core: 2. Of those that a mesh axis runs over, the one named last changes fastest.
Arguments:
- fact_block: int32 [1572864, 1], P(('row', 'col')), may hold values from 0 to 511; in each aligned block of 3072 rows (0 to 3071, 3072 to 6143, ...) at most 12 rows name the same one
- fact_offset: int32 [1572864], P(('row', 'col')), may hold values from 0 to 2047
- fact_date: int32 [1572864], P(('row', 'col')), may hold values from 0 to 2555
- revenue: bfloat16 [1572864], P(('row', 'col')), may hold values from 0.5 to 4
- supplier_words: int32 [35328], P('col'), may hold values from 0 to 1073741823
- date_words: int32 [96], P('col'), may hold values from 0 to 1073741823
- candidates: int32 [1024], replicated, may hold values from 0 to 1048575
Outputs:
- supplier_revenue: float32 [1048576], P(('row', 'col'))
- candidate_revenue: float32 [1024], replicated
- candidate_total: float32 [], replicated
Inputs may be any that keep to these rules, and one draw needn't show every extreme that they name: `fact_block`: each device's rows name no owner block more than 12 times. `candidates`: ids may repeat.
All inputs are finite; a program needn't handle non-finite values.
Results may differ from a plain program's by a relative error of at most 0.0003.
Values sent between devices are 32-bit elements; how exact they have to be, the bound alone decides.
No kernel may reach another device: no remote copies, remote signals or barrier semaphores. Data moves between devices by JAX's collectives and lax.ppermute only.
A program may use at most 64 MiB of HBM per device.

v0:
```python
import jax
import jax.numpy as jnp
from jax import lax
from jax.sharding import Mesh
from jax.sharding import PartitionSpec as P

SUP_DEV = 2048
ROW = ("row_0", "row_1")
COL = ("col_0", "col_1", "col_2")
ROW_COL = ("row_0", "row_1", "col_0", "col_1", "col_2")


def copy_for_each(x, axis):
    copies = jnp.broadcast_to(x, (lax.axis_size(axis), *x.shape))
    return lax.all_to_all(copies, axis, split_axis=0, concat_axis=0, tiled=True)


def joined_along(parts, dim):
    lengths = list(parts.shape[1:])
    lengths[dim] *= parts.shape[0]
    return jnp.moveaxis(parts, 0, dim).reshape(lengths)


def gather_directly(x, axis, dim):
    parts = copy_for_each(x, axis)
    return joined_along(parts, dim)


def over_axes(x, axes):
    for axis in axes:
        x = lax.psum(x, axis)
    return x


def filtered_revenue(owner, fact_offset, fact_date, revenue, supplier_all, date_all):
    words_per_block = (SUP_DEV + 29) // 30
    word_index = owner * words_per_block + fact_offset // 30
    supplier_word = jnp.take(supplier_all, word_index)
    supplier_bit = jnp.bitwise_and(jnp.right_shift(supplier_word, fact_offset % 30), 1)
    date_slot = fact_date // 30
    positions = jnp.arange(date_all.shape[0], dtype=jnp.int32)
    date_word = jnp.sum(
        jnp.where(date_slot[:, None] == positions[None, :], date_all[None, :], 0), axis=1
    )
    date_bit = jnp.bitwise_and(jnp.right_shift(date_word, fact_date % 30), 1)
    return jnp.where(supplier_bit * date_bit == 1, revenue, jnp.zeros_like(revenue))


def per_device(fact_block, fact_offset, fact_date, revenue, supplier_words, date_words, candidates):
    devices = lax.axis_size(ROW) * lax.axis_size(COL)
    supplier_all, date_all = (
        gather_directly(supplier_words, COL, 0),
        gather_directly(date_words, COL, 0),
    )
    owner = fact_block[:, 0]
    masked = filtered_revenue(owner, fact_offset, fact_date, revenue, supplier_all, date_all)
    row_count = fact_offset.shape[0]
    capacity = max(2, 2 * row_count // devices)
    row_ids = jnp.arange(row_count, dtype=jnp.int32)
    earlier = (owner[:, None] == owner[None, :]) & (row_ids[None, :] < row_ids[:, None])
    ranking = jnp.sum(earlier, axis=1, dtype=jnp.int32)
    slot_index = owner * capacity + ranking
    slot_revenue = (
        jnp.zeros((devices * capacity,), jnp.float32).at[slot_index].set(masked.astype(jnp.float32))
    )
    slot_offset = (
        jnp.zeros((devices * capacity,), jnp.float32)
        .at[slot_index]
        .set(fact_offset.astype(jnp.float32))
    )
    payload = jnp.stack((slot_revenue, slot_offset), axis=-1)
    payload = payload.reshape(lax.axis_size(ROW), lax.axis_size(COL), 2 * capacity)
    arrived = lax.all_to_all(
        lax.all_to_all(payload, COL, split_axis=1, concat_axis=1, tiled=True),
        ROW,
        split_axis=0,
        concat_axis=0,
        tiled=True,
    )
    arrived = arrived.reshape(-1, 2)
    owned = jax.ops.segment_sum(
        arrived[:, 0], arrived[:, 1].astype(jnp.int32), num_segments=SUP_DEV
    )
    global_id = owner * SUP_DEV + fact_offset
    onehot_cands = (global_id[:, None] == candidates[None, :]).astype(jnp.bfloat16)
    own_terms = jnp.dot(masked[None, :], onehot_cands, preferred_element_type=jnp.float32)[0]
    candidate_revenue = over_axes(own_terms, ROW_COL)
    candidate_total = jnp.sum(candidate_revenue)
    return (owned, candidate_revenue, candidate_total)


def solution(mesh):
    split = Mesh(mesh.devices.reshape(2, 8, 2, 8, 2), ("row_0", "row_1", "col_0", "col_1", "col_2"))
    return jax.shard_map(
        per_device,
        mesh=split,
        in_specs=(P(ROW_COL, None), P(ROW_COL), P(ROW_COL), P(ROW_COL), P(COL), P(COL), P()),
        out_specs=(P(ROW_COL), P(), P()),
        check_vma=False,
    )
```

profile of v0, /device:TPU:1, one launch (start us, length us, event | category | flops | bytes accessed | tf_op | source)
XLA Modules:
  0.0 199.4 jit_solution(4576482019518081585)
XLA Ops:
  0.6 1.3 broadcast_in_dim.48
  1.9 12.9 %all-to-all-start.1 = ((s32[32,1,3]{2,1,0:T(1,128)}), s32[32,1,3]{2,1,0:T(1,128)S(1)}, u32[]{:S(2)}, u32[]{:S(2)}) async-start(s32[32,1,3]{2,1,0:T(1,128)} %broadcast_in_dim.48), calls=%async_computation.1 | async-start | bytes 32768 | tf_op jit(solution)/shard_map/all_to_all | solution.py:15
  14.8 3.9 %convert_reduce_fusion = s32[3072]{0:T(1024)S(1)} fusion(s32[3072]{0:T(1024)} %bitcast.19), kind=kLoop, calls=%fused_computation.4 | loop fusion | flops 47182848 | bytes 24576 | tf_op jit(solution)/shard_map/reduce_sum | solution.py:61
  18.6 0.7 compare_select_fusion
  19.4 0.8 multiply_add_fusion
  20.2 11.8 %scatter_custom_fusion.1 = f32[6144]{0:T(1024)S(1)} fusion(s32[3072]{0:T(1024)S(1)} %bitcast.24, f32[3072]{0:T(1024)S(1)} %get-tuple-element.7, f32[]{:T(128)} %constant.30.clone.1), kind=kCustom, calls=%fused_computation.33 | custom fusion | bytes 24580 | tf_op jit(solution)/shard_map/scatter | solution.py:69
  32.0 1.4 broadcast_in_dim.45
  33.4 8.3 %all-to-all-start = ((s32[32,1,1104]{2,1,0:T(1,128)}), s32[32,1,1104]{2,1,0:T(1,128)S(1)}, u32[]{:S(2)}, u32[]{:S(2)}) async-start(s32[32,1,1104]{2,1,0:T(1,128)} %broadcast_in_dim.45), calls=%async_computation | async-start | bytes 294912 | tf_op jit(solution)/shard_map/all_to_all | solution.py:15
  41.8 0.7 add_select_fusion.1
  42.5 0.5 broadcast.67
  43.0 0.7 reduce.8
  43.7 0.1 broadcast_in_dim.49
  43.8 0.3 select_reduce_fusion
  44.1 7.0 %all-to-all-done = s32[32,1,1104]{2,1,0:T(1,128)S(1)} async-done(((s32[32,1,1104]{2,1,0:T(1,128)}), s32[32,1,1104]{2,1,0:T(1,128)S(1)}, u32[]{:S(2)}, u32[]{:S(2)}) %all-to-all-start) | async-done | bytes 141344 | tf_op jit(solution)/shard_map/all_to_all | solution.py:15
  51.1 0.3 reduce
  51.4 0.1 reshape.40
  51.5 0.0 copy-start
  51.6 0.0 copy-start.1
  51.6 0.0 copy-start.4
  51.6 17.4 %gather_fusion = s32[3072]{0:T(1024)S(1)} fusion(s32[35328]{0:T(1024)S(1)} %reshape.40, s32[3072]{0:T(1024)S(1)} %get-tuple-element.6), kind=kCustom, calls=%fused_computation | custom fusion | bytes 36864 | tf_op jit(solution)/shard_map/jit(_take)/gather | solution.py:38
  69.1 11.8 %scatter_custom_fusion = f32[6144]{0:T(1024)S(1)} fusion(s32[3072]{0:T(1024)S(1)} %bitcast.25, f32[3072]{0:T(1024)S(1)} %get-tuple-element.3, f32[]{:T(128)} %constant.30.clone.1), kind=kCustom, calls=%fused_computation.35 | custom fusion | bytes 24580 | tf_op jit(solution)/shard_map/scatter | solution.py:64
  81.0 1.1 copy.15
  82.0 0.0 copy-start.5
  82.0 0.8 reshape.41
  82.9 0.2 copy.20
  83.0 0.8 reshape.96
  83.9 5.2 %all-to-all-start.2 = ((f32[32,1,384]{2,1,0:T(1,128)}), f32[32,1,384]{2,1,0:T(1,128)S(1)}, u32[]{:S(2)}, u32[]{:S(2)}) async-start(f32[32,1,384]{2,1,0:T(1,128)} %reshape.96), calls=%async_computation.2 | async-start | bytes 98304 | tf_op jit(solution)/shard_map/all_to_all | solution.py:74
  89.1 8.1 %all-to-all-done.2 = f32[32,1,384]{2,1,0:T(1,128)S(1)} async-done(((f32[32,1,384]{2,1,0:T(1,128)}), f32[32,1,384]{2,1,0:T(1,128)S(1)}, u32[]{:S(2)}, u32[]{:S(2)}) %all-to-all-start.2) | async-done | bytes 49184 | tf_op jit(solution)/shard_map/all_to_all | solution.py:74
  97.2 0.5 broadcast.70
  97.7 0.8 reduce.9
  98.4 0.2 reshape.97
  98.6 0.2 copy.17
  98.8 0.8 reshape.98
  99.5 9.1 %all-to-all-start.3 = ((f32[16,1,768]{2,1,0:T(1,128)}), f32[16,1,768]{2,1,0:T(1,128)S(1)}, u32[]{:S(2)}, u32[]{:S(2)}) async-start(f32[16,1,768]{2,1,0:T(1,128)} %reshape.98), calls=%async_computation.3 | async-start | bytes 98304 | tf_op jit(solution)/shard_map/all_to_all | solution.py:73
  108.7 2.0 %fusion.1 = f32[1,1024]{1,0:T(1,128)S(1)} fusion(bf16[3072,1]{0,1:T(2,128)(2,1)S(1)} %reshape.76, s32[1024]{0:T(1024)S(1)} %copy-done.5, s32[3072]{0:T(1024)S(1)} %get-tuple-element.5), kind=kOutput, calls=%fused_computation.7 | convolution fusion | flops 9437184 | bytes 26624 | tf_op jit(solution)/shard_map/dot_general | solution.py:86
  110.7 5.6 %psum.35 = f32[1024]{0:T(1024)S(1)} all-reduce(f32[1024]{0:T(1024)S(1)} %bitcast.27), channel_id=1, replica_groups=mesh['row_0'=2,'row_1'=8,'col_0'=2,'col_1'=8,'col_2'=2] {'row_0'}, use_global_device_ids=true, to_apply=%region_5.6 | all-reduce | flops 1024 | bytes 8192 | tf_op jit(solution)/shard_map/psum | solution.py:31
  116.2 13.2 %psum.36 = f32[1024]{0:T(1024)S(1)} all-reduce(f32[1024]{0:T(1024)S(1)} %psum.35), channel_id=1, replica_groups=mesh['row_0'=2,'row_1'=8,'col_0'=2,'col_1'=8,'col_2'=2] {'row_1'}, use_global_device_ids=true, to_apply=%region_6.7 | all-reduce | flops 1024 | bytes 8192 | tf_op jit(solution)/shard_map/psum | solution.py:31
  129.4 3.8 %psum.37 = f32[1024]{0:T(1024)S(1)} all-reduce(f32[1024]{0:T(1024)S(1)} %psum.36), channel_id=1, replica_groups=mesh['row_0'=2,'row_1'=8,'col_0'=2,'col_1'=8,'col_2'=2] {'col_0'}, use_global_device_ids=true, to_apply=%region_7.8 | all-reduce | flops 1024 | bytes 8192 | tf_op jit(solution)/shard_map/psum | solution.py:31
  133.2 11.3 %psum.38 = f32[1024]{0:T(1024)S(1)} all-reduce(f32[1024]{0:T(1024)S(1)} %psum.37), channel_id=1, replica_groups=mesh['row_0'=2,'row_1'=8,'col_0'=2,'col_1'=8,'col_2'=2] {'col_1'}, use_global_device_ids=true, to_apply=%region_8.9 | all-reduce | flops 1024 | bytes 8192 | tf_op jit(solution)/shard_map/psum | solution.py:31
  144.5 12.9 %psum.39 = f32[1024]{0:T(1024)S(1)} all-reduce(f32[1024]{0:T(1024)S(1)} %psum.38), channel_id=1, replica_groups=mesh['row_0'=2,'row_1'=8,'col_0'=2,'col_1'=8,'col_2'=2] {'col_2'}, use_global_device_ids=true, to_apply=%region_9.10 | all-reduce | flops 1024 | bytes 8192 | tf_op jit(solution)/shard_map/psum | solution.py:31
  157.4 0.6 reduce_sum.32
  158.0 0.8 reduce.10
  158.8 0.1 reshape.99
  158.9 0.1 copy.18
  159.0 0.8 reshape.42
  159.9 0.9 slice_reduce_fusion
  160.8 1.7 fusion.5
  162.5 36.9 %scatter_custom_fusion.2 = f32[2048]{0:T(1024)} fusion(s32[6144]{0:T(1024)S(1)} %fusion.5, f32[6144]{0:T(1024)S(1)} %slice_reduce_fusion, f32[]{:T(128)} %constant.30.clone.1), kind=kCustom, calls=%fused_computation.43 | custom fusion | flops 6144 | bytes 8196 | tf_op jit(solution)/shard_map/scatter-add | solution.py:81
  (13 shorter events, 0.1 us)
Async XLA Ops:
  1.9 30.1 %all-to-all-start.1 = ((s32[32,1,3]{2,1,0:T(1,128)}), s32[32,1,3]{2,1,0:T(1,128)S(1)}, u32[]{:S(2)}, u32[]{:S(2)}) async-start(s32[32,1,3]{2,1,0:T(1,128)} %broadcast_in_dim.48), calls=%async_computation.1 | async-start | bytes 32768 | tf_op jit(solution)/shard_map/all_to_all | solution.py:15
  33.4 17.6 %all-to-all-start = ((s32[32,1,1104]{2,1,0:T(1,128)}), s32[32,1,1104]{2,1,0:T(1,128)S(1)}, u32[]{:S(2)}, u32[]{:S(2)}) async-start(s32[32,1,1104]{2,1,0:T(1,128)} %broadcast_in_dim.45), calls=%async_computation | async-start | bytes 294912 | tf_op jit(solution)/shard_map/all_to_all | solution.py:15
  51.5 17.5 %copy-start = (s32[3072,1]{0,1:T(1,128)S(1)}, s32[3072,1]{0,1:T(1,128)}, u32[]{:S(2)}) copy-start(s32[3072,1]{0,1:T(1,128)} %param.7) | copy-start | bytes 36868
  51.6 17.5 %copy-start.1 = (s32[3072]{0:T(1024)S(1)}, s32[3072]{0:T(1024)}, u32[]{:S(2)}) copy-start(s32[3072]{0:T(1024)} %param.9) | copy-start | bytes 36868
  51.6 17.5 %copy-start.2 = (s32[3072]{0:T(1024)S(1)}, s32[3072]{0:T(1024)}, u32[]{:S(2)}) copy-start(s32[3072]{0:T(1024)} %param.8) | copy-start | bytes 36868
  51.6 17.5 %copy-start.4 = (bf16[3072]{0:T(1024)(128)(2,1)S(1)}, bf16[3072]{0:T(1024)(128)(2,1)}, u32[]{:S(2)}) copy-start(bf16[3072]{0:T(1024)(128)(2,1)} %param.10) | copy-start | bytes 18436
  82.0 26.6 %copy-start.5 = (s32[1024]{0:T(1024)S(1)}, s32[1024]{0:T(1024)}, u32[]{:S(2)}) copy-start(s32[1024]{0:T(1024)} %param.13) | copy-start | bytes 12292
  83.9 13.3 %all-to-all-start.2 = ((f32[32,1,384]{2,1,0:T(1,128)}), f32[32,1,384]{2,1,0:T(1,128)S(1)}, u32[]{:S(2)}, u32[]{:S(2)}) async-start(f32[32,1,384]{2,1,0:T(1,128)} %reshape.96), calls=%async_computation.2 | async-start | bytes 98304 | tf_op jit(solution)/shard_map/all_to_all | solution.py:74
  99.5 58.5 %all-to-all-start.3 = ((f32[16,1,768]{2,1,0:T(1,128)}), f32[16,1,768]{2,1,0:T(1,128)S(1)}, u32[]{:S(2)}, u32[]{:S(2)}) async-start(f32[16,1,768]{2,1,0:T(1,128)} %reshape.98), calls=%async_computation.3 | async-start | bytes 98304 | tf_op jit(solution)/shard_map/all_to_all | solution.py:73
  157.4 3.4 %copy-start.3 = (f32[1024]{0:T(1024)}, f32[1024]{0:T(1024)S(1)}, u32[]{:S(2)}) copy-start(f32[1024]{0:T(1024)S(1)} %psum.39) | copy-start | bytes 12292
where the time goes:
time: 200 us; the launch traced here: 199 us
  local copies, waits for them, and re-layouts  50.9 us (25%)
  other arithmetic  48.3 us (24%)
  blocking collectives  46.8 us (23%)
  starting transfers between devices  35.5 us (18%)
  waiting for transfers between devices  15.1 us (8%)
  matrix products  2.01 us (1%)
    psum x5, blocking collectives, over_axes(): x = lax.psum(x, axis)  46.8 us
    scatter-add x1, other arithmetic, per_device(): jax.ops.segment_sum(arrived[:, 0], arrived[:, 1].astype(jnp.int32), num_s...  36.9 us
    all_to_all x2, starting transfers between devices, copy_for_each(): return lax.all_to_all(copies, axis, split_axis=0, concat_axis=0, tiled=True)  21.2 us
    gather x1, local copies, waits for them, and re-layouts, filtered_revenue(): supplier_word = jnp.take(supplier_all, word_index)  17.4 us
    scatter x1, local copies, waits for them, and re-layouts, per_device(): jnp.zeros((devices * capacity,), jnp.float32).at[slot_index]  11.8 us
    scatter x1, local copies, waits for them, and re-layouts, per_device(): slot_offset = jnp.zeros((devices * capacity,), jnp.float32).at[slot_index...  11.8 us
    all_to_all x1, starting transfers between devices, per_device(): lax.all_to_all(lax.all_to_all(payload, COL, split_axis=1, concat_axis=1,...  9.1 us
    all_to_all x1, waiting for transfers between devices, per_device(): lax.all_to_all(payload, COL, split_axis=1, concat_axis=1, tiled=True)  8.08 us
  transfers between devices with their start and end apart: 4, of which 2 were waited for; matrix products, arithmetic and copies ran while one was open for 11% of the time, Pallas kernels for 0%

commit v1 on v0

--- a/solution.py
+++ b/solution.py
@@ -28,7 +28,7 @@
 
 def over_axes(x, axes):
     for axis in axes:
-        x = lax.psum(x, axis)
+        x = jnp.sum(lax.all_gather(x, axis), axis=0)
     return x
 
 

time: 200 us -> 218 us (1.090)
  blocking collectives: 46.8 us -> 63.7 us
    all_gather x0 -> x5, blocking collectives: none -> 63.7 us  [over_axes(): x = jnp.sum(lax.all_gather(x, axis), axis=0)]
    psum x5 -> x0, blocking collectives: 46.8 us -> none  [over_axes(): x = lax.psum(x, axis)]
where the time goes in v1:
time: 218 us; the launch traced here: 217 us
  blocking collectives  63.7 us (29%)
  local copies, waits for them, and re-layouts  51 us (23%)
  other arithmetic  48.9 us (22%)
  starting transfers between devices  35.5 us (16%)
  waiting for transfers between devices  15.1 us (7%)
    all_gather x5, blocking collectives, over_axes(): x = jnp.sum(lax.all_gather(x, axis), axis=0)  63.7 us
    scatter-add x1, other arithmetic, per_device(): jax.ops.segment_sum(arrived[:, 0], arrived[:, 1].astype(jnp.int32), num_s...  36.9 us
    all_to_all x2, starting transfers between devices, copy_for_each(): return lax.all_to_all(copies, axis, split_axis=0, concat_axis=0, tiled=True)  21.2 us
    gather x1, local copies, waits for them, and re-layouts, filtered_revenue(): supplier_word = jnp.take(supplier_all, word_index)  17.4 us
    scatter x1, local copies, waits for them, and re-layouts, per_device(): slot_offset = jnp.zeros((devices * capacity,), jnp.float32).at[slot_index...  11.8 us
    scatter x1, local copies, waits for them, and re-layouts, per_device(): jnp.zeros((devices * capacity,), jnp.float32).at[slot_index]  11.8 us
    all_to_all x1, starting transfers between devices, per_device(): lax.all_to_all(lax.all_to_all(payload, COL, split_axis=1, concat_axis=1,...  9.1 us
    all_to_all x1, waiting for transfers between devices, per_device(): lax.all_to_all(payload, COL, split_axis=1, concat_axis=1, tiled=True)  8.08 us
  transfers between devices with their start and end apart: 4, of which 2 were waited for; matrix products, arithmetic and copies ran while one was open for 11% of the time, Pallas kernels for 0%

profile of v1, /device:TPU:1, one launch (start us, length us, event | category | flops | bytes accessed | tf_op | source)
XLA Modules:
  0.0 217.1 jit_solution(10935652144097117320)
XLA Ops:
  0.6 1.3 broadcast_in_dim.48
  1.9 12.9 %all-to-all-start.1 = ((s32[32,1,3]{2,1,0:T(1,128)}), s32[32,1,3]{2,1,0:T(1,128)S(1)}, u32[]{:S(2)}, u32[]{:S(2)}) async-start(s32[32,1,3]{2,1,0:T(1,128)} %broadcast_in_dim.48), calls=%async_computation.1 | async-start | bytes 32768 | tf_op jit(solution)/shard_map/all_to_all | solution.py:15
  14.8 3.9 %convert_reduce_fusion = s32[3072]{0:T(1024)S(1)} fusion(s32[3072]{0:T(1024)} %bitcast.19), kind=kLoop, calls=%fused_computation.4 | loop fusion | flops 47182848 | bytes 24576 | tf_op jit(solution)/shard_map/reduce_sum | solution.py:61
  18.6 0.7 compare_select_fusion
  19.4 0.8 multiply_add_fusion
  20.2 11.8 %scatter_custom_fusion.1 = f32[6144]{0:T(1024)S(1)} fusion(s32[3072]{0:T(1024)S(1)} %bitcast.24, f32[3072]{0:T(1024)S(1)} %get-tuple-element.7, f32[]{:T(128)} %constant.30.clone.1), kind=kCustom, calls=%fused_computation.33 | custom fusion | bytes 24580 | tf_op jit(solution)/shard_map/scatter | solution.py:69
  32.0 1.4 broadcast_in_dim.45
  33.4 8.3 %all-to-all-start = ((s32[32,1,1104]{2,1,0:T(1,128)}), s32[32,1,1104]{2,1,0:T(1,128)S(1)}, u32[]{:S(2)}, u32[]{:S(2)}) async-start(s32[32,1,1104]{2,1,0:T(1,128)} %broadcast_in_dim.45), calls=%async_computation | async-start | bytes 294912 | tf_op jit(solution)/shard_map/all_to_all | solution.py:15
  41.8 0.7 add_select_fusion.1
  42.5 0.5 broadcast.67
  43.0 0.7 reduce.10
  43.7 0.1 broadcast_in_dim.49
  43.8 0.3 select_reduce_fusion
  44.1 7.0 %all-to-all-done = s32[32,1,1104]{2,1,0:T(1,128)S(1)} async-done(((s32[32,1,1104]{2,1,0:T(1,128)}), s32[32,1,1104]{2,1,0:T(1,128)S(1)}, u32[]{:S(2)}, u32[]{:S(2)}) %all-to-all-start) | async-done | bytes 141344 | tf_op jit(solution)/shard_map/all_to_all | solution.py:15
  51.1 0.3 reduce.2
  51.4 0.1 reshape.39
  51.5 0.0 copy-start
  51.6 0.0 copy-start.3
  51.6 17.4 %gather_fusion = s32[3072]{0:T(1024)S(1)} fusion(s32[35328]{0:T(1024)S(1)} %reshape.39, s32[3072]{0:T(1024)S(1)} %get-tuple-element.6), kind=kCustom, calls=%fused_computation | custom fusion | bytes 36864 | tf_op jit(solution)/shard_map/jit(_take)/gather | solution.py:38
  69.1 11.8 %scatter_custom_fusion = f32[6144]{0:T(1024)S(1)} fusion(s32[3072]{0:T(1024)S(1)} %bitcast.25, f32[3072]{0:T(1024)S(1)} %get-tuple-element.3, f32[]{:T(128)} %constant.30.clone.1), kind=kCustom, calls=%fused_computation.35 | custom fusion | bytes 24580 | tf_op jit(solution)/shard_map/scatter | solution.py:64
  81.0 1.1 copy.15
  82.0 0.0 copy-start.4
  82.0 0.8 reshape.40
  82.9 0.2 copy.20
  83.0 0.8 reshape.100
  83.9 5.2 %all-to-all-start.2 = ((f32[32,1,384]{2,1,0:T(1,128)}), f32[32,1,384]{2,1,0:T(1,128)S(1)}, u32[]{:S(2)}, u32[]{:S(2)}) async-start(f32[32,1,384]{2,1,0:T(1,128)} %reshape.100), calls=%async_computation.2 | async-start | bytes 98304 | tf_op jit(solution)/shard_map/all_to_all | solution.py:74
  89.1 8.1 %all-to-all-done.2 = f32[32,1,384]{2,1,0:T(1,128)S(1)} async-done(((f32[32,1,384]{2,1,0:T(1,128)}), f32[32,1,384]{2,1,0:T(1,128)S(1)}, u32[]{:S(2)}, u32[]{:S(2)}) %all-to-all-start.2) | async-done | bytes 49184 | tf_op jit(solution)/shard_map/all_to_all | solution.py:74
  97.2 0.5 broadcast.70
  97.7 0.8 reduce.11
  98.4 0.2 reshape.101
  98.6 0.2 copy.17
  98.8 0.8 reshape.102
  99.5 9.1 %all-to-all-start.3 = ((f32[16,1,768]{2,1,0:T(1,128)}), f32[16,1,768]{2,1,0:T(1,128)S(1)}, u32[]{:S(2)}, u32[]{:S(2)}) async-start(f32[16,1,768]{2,1,0:T(1,128)} %reshape.102), calls=%async_computation.3 | async-start | bytes 98304 | tf_op jit(solution)/shard_map/all_to_all | solution.py:73
  108.7 2.0 fusion.1
  110.7 4.9 %all-gather = f32[2048]{0:T(1024)S(1)} all-gather(f32[1024]{0:T(1024)S(1)} %bitcast.27), channel_id=2, replica_groups=mesh['row_0'=2,'row_1'=8,'col_0'=2,'col_1'=8,'col_2'=2] {'row_0'}, dimensions={0}, use_global_device_ids=true | all-gather | bytes 12288 | tf_op jit(solution)/shard_map/all_gather | solution.py:31
  115.6 19.4 %all-gather.1 = f32[8192]{0:T(1024)S(1)} all-gather(f32[1024]{0:T(1024)S(1)} %reduce_sum.77), channel_id=3, replica_groups=mesh['row_0'=2,'row_1'=8,'col_0'=2,'col_1'=8,'col_2'=2] {'row_1'}, dimensions={0}, use_global_device_ids=true | all-gather | bytes 36864 | tf_op jit(solution)/shard_map/all_gather | solution.py:31
  135.0 3.2 %all-gather.2 = f32[2048]{0:T(1024)S(1)} all-gather(f32[1024]{0:T(1024)S(1)} %reduce_sum.78), channel_id=4, replica_groups=mesh['row_0'=2,'row_1'=8,'col_0'=2,'col_1'=8,'col_2'=2] {'col_0'}, dimensions={0}, use_global_device_ids=true | all-gather | bytes 12288 | tf_op jit(solution)/shard_map/all_gather | solution.py:31
  138.3 18.3 %all-gather.3 = f32[8192]{0:T(1024)S(1)} all-gather(f32[1024]{0:T(1024)S(1)} %reduce_sum.79), channel_id=5, replica_groups=mesh['row_0'=2,'row_1'=8,'col_0'=2,'col_1'=8,'col_2'=2] {'col_1'}, dimensions={0}, use_global_device_ids=true | all-gather | bytes 36864 | tf_op jit(solution)/shard_map/all_gather | solution.py:31
  156.6 17.9 %all-gather.4 = f32[2048]{0:T(1024)S(1)} all-gather(f32[1024]{0:T(1024)S(1)} %reduce_sum.80), channel_id=6, replica_groups=mesh['row_0'=2,'row_1'=8,'col_0'=2,'col_1'=8,'col_2'=2] {'col_2'}, dimensions={0}, use_global_device_ids=true | all-gather | bytes 12288 | tf_op jit(solution)/shard_map/all_gather | solution.py:31
  174.5 0.6 reduce_sum.82
  175.1 0.6 reduce_sum.81
  175.7 0.8 reduce.12
  176.4 0.1 reshape.103
  176.6 0.1 copy.18
  176.7 0.8 reshape.41
  177.5 0.9 slice_reduce_fusion
  178.4 1.7 fusion.5
  180.1 36.9 %scatter_custom_fusion.2 = f32[2048]{0:T(1024)} fusion(s32[6144]{0:T(1024)S(1)} %fusion.5, f32[6144]{0:T(1024)S(1)} %slice_reduce_fusion, f32[]{:T(128)} %constant.30.clone.1), kind=kCustom, calls=%fused_computation.43 | custom fusion | flops 6144 | bytes 8196 | tf_op jit(solution)/shard_map/scatter-add | solution.py:81
  (21 shorter events, 0.2 us)
Async XLA Ops:
  1.9 30.1 %all-to-all-start.1 = ((s32[32,1,3]{2,1,0:T(1,128)}), s32[32,1,3]{2,1,0:T(1,128)S(1)}, u32[]{:S(2)}, u32[]{:S(2)}) async-start(s32[32,1,3]{2,1,0:T(1,128)} %broadcast_in_dim.48), calls=%async_computation.1 | async-start | bytes 32768 | tf_op jit(solution)/shard_map/all_to_all | solution.py:15
  33.4 17.6 %all-to-all-start = ((s32[32,1,1104]{2,1,0:T(1,128)}), s32[32,1,1104]{2,1,0:T(1,128)S(1)}, u32[]{:S(2)}, u32[]{:S(2)}) async-start(s32[32,1,1104]{2,1,0:T(1,128)} %broadcast_in_dim.45), calls=%async_computation | async-start | bytes 294912 | tf_op jit(solution)/shard_map/all_to_all | solution.py:15
  51.5 17.5 %copy-start = (s32[3072,1]{0,1:T(1,128)S(1)}, s32[3072,1]{0,1:T(1,128)}, u32[]{:S(2)}) copy-start(s32[3072,1]{0,1:T(1,128)} %param.7) | copy-start | bytes 36868
  51.6 17.5 %copy-start.1 = (s32[3072]{0:T(1024)S(1)}, s32[3072]{0:T(1024)}, u32[]{:S(2)}) copy-start(s32[3072]{0:T(1024)} %param.9) | copy-start | bytes 36868
  51.6 17.5 %copy-start.2 = (s32[3072]{0:T(1024)S(1)}, s32[3072]{0:T(1024)}, u32[]{:S(2)}) copy-start(s32[3072]{0:T(1024)} %param.8) | copy-start | bytes 36868
  51.6 17.5 %copy-start.3 = (bf16[3072]{0:T(1024)(128)(2,1)S(1)}, bf16[3072]{0:T(1024)(128)(2,1)}, u32[]{:S(2)}) copy-start(bf16[3072]{0:T(1024)(128)(2,1)} %param.10) | copy-start | bytes 18436
  82.0 26.6 %copy-start.4 = (s32[1024]{0:T(1024)S(1)}, s32[1024]{0:T(1024)}, u32[]{:S(2)}) copy-start(s32[1024]{0:T(1024)} %param.13) | copy-start | bytes 12292
  83.9 13.3 %all-to-all-start.2 = ((f32[32,1,384]{2,1,0:T(1,128)}), f32[32,1,384]{2,1,0:T(1,128)S(1)}, u32[]{:S(2)}, u32[]{:S(2)}) async-start(f32[32,1,384]{2,1,0:T(1,128)} %reshape.100), calls=%async_computation.2 | async-start | bytes 98304 | tf_op jit(solution)/shard_map/all_to_all | solution.py:74
  99.5 76.1 %all-to-all-start.3 = ((f32[16,1,768]{2,1,0:T(1,128)}), f32[16,1,768]{2,1,0:T(1,128)S(1)}, u32[]{:S(2)}, u32[]{:S(2)}) async-start(f32[16,1,768]{2,1,0:T(1,128)} %reshape.102), calls=%async_computation.3 | async-start | bytes 98304 | tf_op jit(solution)/shard_map/all_to_all | solution.py:73
